TPU v7x, 32 devices: a whole 2x2x4 slice. The times are simulated.
32 devices in a mesh: ctx: 8 (over y, x, core), tp: 4 (over z).
Axes of the slice: x: 2, y: 2, z: 4, core: 2. Of those that a mesh axis runs over, the one named last changes fastest.
Arguments:
- tokens: bfloat16 [4096, 768], P('ctx'), may hold values from -6 to 6
- cotangent: bfloat16 [4096, 768], P('ctx'), may hold values from -8 to 8
- block_pos: int32 [32], replicated, may hold values from 0 to 15, as said below
- block_seq: int32 [32], replicated, may hold values from 0 to 1, as said below
- ln1_gain: float32 [768], replicated, may hold values from 0.5 to 1.5
- ln1_bias: float32 [768], replicated, may hold values from -1.2 to 1.2
- qkv_weight: bfloat16 [768, 3, 768], P(None, None, 'tp'), may hold values from -5 to 5
- qv_bias: float32 [2, 768], P(None, 'tp'), may hold values from -2.5 to 2.5
- out_weight: bfloat16 [768, 768], P('tp'), may hold values from -6 to 6
- out_bias: float32 [768], replicated, may hold values from -1.2 to 1.2
- ln2_gain: float32 [768], replicated, may hold values from 0.5 to 1.5
- ln2_bias: float32 [768], replicated, may hold values from -1.2 to 1.2
- fc_weight: bfloat16 [768, 3072], P(None, 'tp'), may hold values from -0.4375 to 0.4375
- fc_bias: float32 [3072], P('tp'), may hold values from -2.5 to 2.5
- proj_weight: bfloat16 [3072, 768], P('tp'), may hold values from -0.21875 to 0.21875
- proj_bias: float32 [768], replicated, may hold values from -1.2 to 1.2
Outputs:
- output: bfloat16 [4096, 768], P('ctx')
- grad_tokens: bfloat16 [4096, 768], P('ctx')
- grad_ln1_gain: float32 [768], replicated
- grad_ln1_bias: float32 [768], replicated
- grad_qkv_weight: float32 [768, 3, 768], P(None, None, 'tp')
- grad_qv_bias: float32 [2, 768], P(None, 'tp')
- grad_out_weight: float32 [768, 768], P('tp')
- grad_out_bias: float32 [768], replicated
- grad_ln2_gain: float32 [768], replicated
- grad_ln2_bias: float32 [768], replicated
- grad_fc_weight: float32 [768, 3072], P(None, 'tp')
- grad_fc_bias: float32 [3072], P('tp')
- grad_proj_weight: float32 [3072, 768], P('tp')
- grad_proj_bias: float32 [768], replicated
Inputs may be any that keep to these rules, and one draw needn't show every extreme that they name: `block_pos`: block b holds tokens [b * 128, (b+1) * 128) of the whole; each index r of ctx holds blocks 4r to 4r+3, two of each sequence, at positions p and 15 - p; every position of each sequence is held by exactly one block. `block_seq`: two sequences; each index of ctx holds two blocks of each.
All inputs are finite; a program needn't handle non-finite values.
Results may differ from a plain program's by a relative error of at most 0.025.
Values may be sent and summed in bfloat16 or wider, within the bound.
A program may use at most 320 MiB of HBM per device.

v0:
```python
import functools
from types import SimpleNamespace

import jax
import jax.numpy as jnp
from jax import lax
from jax.experimental import pallas as pl
from jax.experimental.pallas import tpu as pltpu
from jax.sharding import PartitionSpec as P

HEAD = 64
BLK = 128

class Names:
    def __getattr__(self, name):
        return name


ID = Names()
BF = jnp.bfloat16
F32 = jnp.float32
MESH = pl.DeviceIdType.MESH
NEG = -1e30
C0 = 0.7978845608028654
C1 = 0.044715
U = 4
SENDS = 90
SPLIT_AT = 26
ARRIVALS = 222
TIDY = (ID.far1, ID.feed1, ID.weights_b, ID.high, ID.low3, ID.collect0, (ID.n1_, 2))

LAT = 1.6
OUT_FROM = 15.0
OUT_GAP = 1.0
DS = (3, 2, 1)


def dg(a, b, ca, cb):
    return lax.dot_general(a, b, (((ca,), (cb,)), ((), ())), preferred_element_type=F32)


def normed(x):
    centre = jnp.mean(x, axis=-1, keepdims=True)
    shifted = x - centre
    spread = jnp.mean(shifted * shifted, axis=-1, keepdims=True)
    inverse = lax.rsqrt(spread + 1e-05)
    return shifted * inverse, inverse


def fold8(x):
    rows, width = x.shape
    return jnp.sum(x.reshape(rows // 8, 8, width), axis=0)


def roll64(x):
    return pltpu.roll(x, 64, 1)


def simulate(T, jobs, marks, lat, order=None):
    free = {}
    seen = [dict() for _ in range(T)]
    inbox = [[] for _ in range(T)]
    now = [0.0] * T
    steps = [dict() for _ in range(T)]
    left = [list(marks) if order is None else list(order) for _ in range(T)]
    out = [[] for _ in range(T)]
    parts = [dict() for _ in range(T)]
    OP = 0.12

    def post(time, z, step, op):
        tau = jobs[op[3]][0][op[2]]
        begin = max(time, free.get((z, step), 0.0))
        free[z, step] = begin + tau
        inbox[z + step].append((begin + tau + lat, op))

    def spread(time, z, op):
        if jobs[op[3]][4]:
            for to in range(T):
                step = 1 if to > z else -1
                begin = time
                for k in range(z, to, step):
                    begin = max(begin + (0.7 if k != z else 0.0), free.get((k, step), 0.0))
                    free[k, step] = begin + jobs[op[3]][0][op[2]]
                if to != z:
                    inbox[to].append((begin + jobs[op[3]][0][op[2]] + lat, op))
            return
        if z >= op[1] and z < T - 1:
            post(time, z, 1, op)
        if z <= op[1] and z > 0:
            post(time, z, -1, op)

    def passive(z, op):
        kind, i, u, name = op
        if kind in (ID.R, ID.L):
            return i == z
        return jobs[name][4] or (z in (0, T - 1) and jobs[name][2])

    def start_of(z, item):
        if item[0] == ID.op:
            time, op = item[1]
            if op[0] in (ID.R, ID.L):
                own = parts[z].get((op[3], op[2]))
                if own is None:
                    return None
                time = max(time, own)
            return max(time, now[z])
        step = marks[item[1]]
        time = max(now[z], step.get(ID.time, 0.0))
        for name, delay in step.get(ID.after, ()):
            if name not in steps[z]:
                return None
            time = max(time, steps[z][name] + delay)
        for event in step.get(ID.needs, ()):
            event = tuple(z if e == ID.z else e for e in event)
            if event[0] in (ID.R, ID.L) and event[1] == (0 if event[0] == ID.R else T - 1):
                continue
            if event[0] == ID.A and event[1] == z:
                continue
            if event not in seen[z]:
                return None
            time = max(time, seen[z][event])
        return time

    while True:
        best = None
        for z in range(T):
            for entry in list(inbox[z]):
                if passive(z, entry[1]):
                    seen[z][entry[1]] = entry[0]
                    inbox[z].remove(entry)
            for entry in inbox[z]:
                time = start_of(z, (ID.op, entry))
                if time is not None:
                    key = (time, 0 if jobs[entry[1][3]][3] == 0 else 1, entry[0], z)
                    if best is None or key < best[0]:
                        best = (key, z, (ID.op, entry))
            choices = left[z][:1] if order is not None else left[z]
            for k, name in enumerate(choices):
                time = start_of(z, (ID.mark, name))
                if time is not None:
                    key = (time + 0.01, 2 + marks[name].get(ID.low, 0), k, z)
                    if best is None or key < best[0]:
                        best = (key, z, (ID.mark, name))
        if best is None:
            break
        key, z, item = best
        begin = start_of(z, item)
        if item[0] == ID.op:
            _, op = item[1]
            inbox[z].remove(item[1])
            out[z].append((begin, item[1][1]))
            now[z] = begin + OP
            if op[0] == ID.A:
                seen[z][op] = begin
                spread(now[z], z, op)
            else:
                post(now[z], z, 1 if op[0] == ID.R else -1, op)
        else:
            name = item[1]
            step = marks[name]
            left[z].remove(name)
            out[z].append((begin, (ID.M, name)))
            now[z] = begin + step[ID.dur]
            steps[z][name] = now[z]
            for job, u, kind in step.get(ID.posts, ()):
                if kind == ID.gather:
                    spread(now[z], z, (ID.A, z, u, job))
                else:
                    parts[z].setdefault((job, u), now[z])
                    for d in kind:
                        if z == 0:
                            post(now[z], z, 1, (ID.R, d, u, job))
                        if z == T - 1:
                            post(now[z], z, -1, (ID.L, T - 1 - d, u, job))
    if order is None:
        spots = {name: sum(t for z in range(T) for t, op in out[z] if op == (ID.M, name)) for name in marks}
        assert all(len(l) == 0 for l in left), left
        return simulate(T, jobs, marks, lat, sorted(marks, key=lambda n: spots[n]))
    assert all(len(l) == 0 for l in left) and all(len(i) == 0 for i in inbox), (left, inbox)
    return out, max(now)

def emit(T, z, timeline, jobs, marks, actors, steps, flush):
    names = [op[1] for _, op in timeline[0] if op[0] == ID.M]
    todo = [[op for _, op in timeline[zz]] for zz in range(T)]
    waited = [set() for _ in range(T)]
    for name in names:
        for zz in range(T):
            now = []
            while todo[zz][0] != (ID.M, name):
                now.append(todo[zz].pop(0))
            todo[zz].pop(0)
            for event in marks[name].get(ID.needs, ()):
                job = jobs.get(event[3])
                if event[0] == ID.A and event[1] != zz and (job[4] or (zz in (0, T - 1) and job[2])):
                    if event not in waited[zz]:
                        waited[zz].add(event)
                        now.append(event)
            if now:
                @pl.when(z == zz)
                def _(now=now, zz=zz):
                    for op in now:
                        actors[op[3]].one(op, zz)
        if name in steps:
            steps[name]()
        if name in TIDY:
            flush()


def timetable(U, T):
    S = U // 2
    tau = 4.18 / U + 0.1
    hi, lo = range(S), range(S, U)
    norm = 0.15 + 0.8 / U
    jobs = {
        ID.wo: ([1.65] * 2, False, True, 0, False), ID.ab: ([1.5] * 2, False, True, 0, False),
        ID.ac: ([0.8] * 2, False, True, 0, False), ID.ga2: ([tau] * U, True, True, 0, False),
        ID.out: ([tau] * U, True, False, 1, False), ID.ga1: ([tau] * U, True, False, 0, False),
        ID.small: ([0.5], False, False, 0, True),
    }
    m = {}

    def step(name, dur, after=(), needs=(), posts=(), low=0, time=0.0):
        m[name] = dict(dur=dur, after=list(after), needs=list(needs), posts=list(posts), low=low, time=time)

    def every(job, pieces):
        return [(ID.A, i, u, job) for i in range(T) for u in pieces]

    step(ID.wo, 0.0, posts=[(ID.wo, 0, ID.gather), (ID.wo, 1, ID.gather)])
    step(ID.go, 0.3, [(ID.wo, 2.2)])
    step(ID.own, 2.4, [(ID.go, 0)])
    step(ID.relay0, 0.1, [(ID.go, 3.3)])
    step(ID.near0, 1.1, [(ID.go, 4.6), (ID.relay0, 0), (ID.own, 0)])
    step(ID.relay1, 0.1, [(ID.go, 6.0), (ID.relay0, 0)])
    step(ID.far0, 1.1, [(ID.relay0, 4.2), (ID.near0, 0)], posts=[(ID.ab, 0, ID.gather)])
    step(ID.near1, 1.1, [(ID.relay1, 2.0), (ID.far0, 0)])
    step(ID.relay2, 0.1, [(ID.relay1, 4.6)])
    step(ID.far1, 1.1, [(ID.relay1, 4.4), (ID.near1, 0)], posts=[(ID.ab, 1, ID.gather)])
    step(ID.upstream, 0.8, [(ID.far1, 0)])
    step(ID.near2, 1.1, [(ID.relay2, 2.0), (ID.upstream, 0)])
    step(ID.far2, 1.2, [(ID.relay2, 4.0), (ID.near2, 0)], posts=[(ID.ac, 0, ID.gather), (ID.ac, 1, ID.gather)])
    step(ID.pads, 0.4, [(ID.far2, 0)], every(ID.wo, [0, 1]))
    step(ID.mix, 1.0, [(ID.pads, 0)], every(ID.ab, [0, 1]))
    step(ID.feed1, 3.1, [(ID.mix, 0)], every(ID.ac, [0]), [(ID.ga2, u, DS) for u in hi])
    step(ID.feed0, 3.1, [(ID.feed1, 0)], every(ID.ac, [1]), [(ID.ga2, u, DS) for u in lo])
    step(ID.weights_a, 0.8, [(ID.feed0, 2.0)], low=1)
    step(ID.weights_a2, 0.8, [(ID.weights_a, 0)], low=1)
    step(ID.out_partial, 0.8, [(ID.weights_a2, 2.0)], low=1)
    step(ID.weights_b, 0.4, [(ID.weights_a2, 4.5)], low=1)
    step(ID.near_w1, 0.3, [(ID.weights_b, 5.0)], low=1)
    for u in range(U):
        sums = lambda job: [(ID.R, ID.z, u, job), (ID.L, ID.z, u, job)]
        step((ID.n2_, u), norm, needs=sums(ID.ga2), posts=[(ID.ga2, u, ID.gather)])
        for d in DS:
            step((ID.begin_out, u, d), 0.0, [(ID.out_partial, 0), (ID.feed0, OUT_FROM + OUT_GAP * (3 * u + 3 - d))],
                 posts=[(ID.out, u, (d,))], low=1)
        step((ID.out_, u), 0.2, needs=sums(ID.out), posts=[(ID.out, u, ID.gather)], low=1)
        step((ID.n1_, u), norm, needs=sums(ID.ga1), posts=[(ID.ga1, u, ID.gather)])
    m[(ID.n1_, U - 1)][ID.posts].insert(0, (ID.small, 0, ID.gather))
    step(ID.high, 1.4, needs=every(ID.ga2, hi))
    step(ID.high2, 0.9, [(ID.high, 0)])
    step(ID.near_k1a, 0.15, [(ID.high, 3.4), (ID.high2, 0)])
    step(ID.high3, 0.9, [(ID.high2, 0)])
    step(ID.near_k1b, 0.15, [(ID.near_k1a, 0), (ID.high3, 0)])
    step(ID.mid3, 0.9, [(ID.high3, 0)])
    step(ID.low, 1.4, [(ID.mid3, 0), (ID.near_k1b, 0)], every(ID.ga2, lo))
    step(ID.low2, 1.7, [(ID.low, 0)])
    step(ID.near_k0a, 0.15, [(ID.low, 3.4), (ID.low2, 0)])
    step(ID.low3, 1.7, [(ID.low2, 0)])
    step(ID.near_k0b, 0.15, [(ID.near_k0a, 0), (ID.low3, 0)])
    step(ID.own_hi, 1.7, [(ID.low3, 0)])
    step(ID.collect1, 0.9, [(ID.own_hi, 0), (ID.near_k1b, 7.0)], posts=[(ID.ga1, u, DS) for u in hi])
    step(ID.own_lo, 0.9, [(ID.collect1, 0)])
    step(ID.finish_w1, 0.3, [(ID.near_w1, 8.0), (ID.near_k0b, 0)], low=1)
    step(ID.aw, 0.6, [(ID.own_lo, 0)], low=1)
    step(ID.collect0, 0.9, [(ID.own_lo, 0), (ID.near_k0b, 7.0)], posts=[(ID.ga1, u, DS) for u in lo])
    step(ID.weights_c, 0.7, [(ID.collect0, 0), (ID.aw, 0)], low=1)
    step(ID.weights_d, 0.3, [(ID.weights_c, 3.0)], low=1)
    step(ID.near_w2, 0.2, [(ID.weights_d, 3.5)], low=1)
    step(ID.relay_w1, 0.05, [(ID.finish_w1, 6.5)], low=1)
    step(ID.finish_w2, 0.2, [(ID.near_w2, 5.0)], low=1)
    step(ID.relay_w2, 0.05, [(ID.finish_w2, 4.0)], low=1)
    step(ID.pair_w1, 0.05, [(ID.relay_w1, 5.0)], low=1)
    step(ID.give_w1, 0.05, [(ID.pair_w1, 4.5)], low=1)
    step(ID.give_o, 0.1, [((ID.out_, U - 1), 2.0)], every(ID.out, range(U)), low=1)
    step(ID.sums, 0.2, needs=every(ID.small, [0]), low=1)
    step(ID.pair_w2, 0.05, [(ID.relay_w2, 3.5)], low=1)
    step(ID.give_v, 0.1, [(ID.sums, 3.0)], low=1)
    step(ID.give_w2, 0.05, [(ID.pair_w2, 3.0)], low=1)
    step(ID.give_hi, 0.1, [(ID.give_o, 0)], every(ID.ga1, hi), low=1)
    step(ID.end, 0.0, [(ID.give_v, 0), (ID.give_hi, 0), (ID.give_w1, 0), (ID.give_w2, 0)], every(ID.ga1, range(U)))
    return jobs, m


def scratch_list(R, T, D, F, nh):
    NG = R // 2
    N = 4 * BLK
    v = pltpu.VMEM
    rows = v((8, 64, D), BF)
    return dict(
        tok_raw=(rows),
        cot_raw=(rows),
        stage=(v((2, 2, 2, 64, D), BF)),
        x=(rows),
        cot=(rows),
        wqt=(v((640, D), BF)),
        wo=(v((T, 2, nh * HEAD // 2, D), BF)),
        wolo=(v((nh, T, BLK, D), BF)),
        wohi=(v((nh, T, BLK, D), BF)),
        wopad=(v((nh * BLK, D), BF)),
        fc=(v((D, F), BF)),
        pw=(v((F, D), BF)),
        brow=(v((1, 640), F32)),
        act1=(rows),
        q=(v((nh, N, 128), BF)),
        kv=(v((NG, nh, N, 128), BF)),
        pre=(v((N, D), F32)),
        ga=(v((N, F), F32)),
        hid=(v((8, 64, D), F32)),
        act2=(v((N, D), BF)),
        actd=(v((N, F), BF)),
        gpre=(v((N, F), BF)),
        mlo=(v((4 if NG == 4 else 1, 256, 256), F32)),
        mhi=(v((4 if NG == 4 else 1, 256, 256), F32)),
        m=(v((2 * nh, 1, 256), F32)),
        l=(v((2 * nh, 1, 256), F32)),
        delta=(v((2 * nh, 1, 256), F32)),
        acc=(v((2 * nh, 128, 256), F32)),
        attp=(v((nh, N, 128), BF)),
        attn=(v((N, 256), BF)),
        ab=(v((T, nh, 256, 128), BF)),
        p1=(rows), r1=(rows), l1=(rows),
        r2=(rows), l2=(rows),
        r3=(rows), l3=(rows),
        gh=(v((2, 64, D), F32)),
        h=(rows),
        do=(v((nh, N, 128), BF)),
        dkf=(v((4 if NG == 4 else 1, nh, 256, 128), F32)),
        dk=(v((NG, nh, N, 128), BF)),
        dkr=(v((NG, nh, N, 128), BF)),
        dka=(v((2, 2, nh, 128, 128), BF)),
        gn=(v((N, 640), BF)),
        w1=(v((2, NG, D // NG, D), BF)),
        w1r=(v((NG, D // NG, D), BF)),
        w1s=(v((NG, D // NG, D), BF)),
        w1a=(v((2, D // NG // 2, D), BF)),
        w1f=(v((2, NG, D // NG, D), BF)),
        w2=(v((2, NG, D // 2 // NG, D), BF)),
        w2r=(v((NG, D // 2 // NG, D), BF)),
        w2s=(v((NG, D // 2 // NG, D), BF)),
        w2a=(v((2, D // 2 // NG // 2, D), BF)),
        w2f=(v((2, NG, D // 2 // NG, D), BF)),
        yo=(rows),
        yg=(rows),
        mo=(v((2, 2, 64, D), BF)),
        mg=(v((2, 2, 64, D), BF)),
        vsum=(v((16, D), F32)),
        vz=(v((T, 16, D), BF)),
        vc=(v((R, 16, D), BF)),
        ss=(pltpu.SemaphoreType.DMA((SENDS if NG == 4 else 200,))),
        rs=(pltpu.SemaphoreType.DMA((ARRIVALS if NG == 4 else 400,))),
        ls=(pltpu.SemaphoreType.DMA((24,))),
    )


def layer_kernel(R, T, D, F, nh, names, *refs):
    (pos_ref, seq_ref, tok_hbm, cot_hbm, g1_ref, b1_ref, wqt_hbm, qvb_ref, wo_hbm, ob_ref, g2_ref,
     b2_ref, fc_hbm, fcb_ref, pw_hbm, pb_ref, w1_out, w2_out, fo_out, fg_out, v_out) = refs[:21]
    s = SimpleNamespace(**dict(zip(names, refs[21:])))
    s.p2, s.p3 = s.tok_raw, s.cot_raw
    NG = R // 2
    N = 4 * BLK
    Q1 = D // NG
    Q2 = D // 2 // NG
    SUB = U // 2
    RU = 64 // SUB
    r = lax.axis_index("ctx")
    z = lax.axis_index("tp")
    c = lax.rem(r, 2)
    o = 1 - c
    g = lax.div(r, 2)
    mate = 2 * g + o
    zp, zm = z + 1, z - 1
    not_core = [c != 0, c != 1]
    if NG == 4:
        ga_ = g + 1 - 2 * lax.rem(g, 2)
        gb_ = g + 2 - 4 * lax.div(g, 2)
        gc_ = ga_ + 2 - 4 * lax.div(ga_, 2)
        peers = [g, ga_, gb_, gc_]
        sources = peers
    else:
        peers = [lax.rem(g + t, NG) for t in range(NG)]
        sources = [lax.rem(g + NG - t, NG) for t in range(NG)]

    most = {ID.common: 0, ID.line: 0}
    spare = {ID.common: [], 0: [], 1: [], 2: [], 3: []}
    started = [[], []]
    ids = [0]
    SPLIT = SPLIT_AT if NG == 4 else 100

    def take(pool):
        if spare[pool]:
            return spare[pool].pop(0)
        kind = ID.common if pool == ID.common else pool
        most[kind] = most.get(kind, 0) + 1
        return most[kind] - 1 + (0 if pool == ID.common else SPLIT)

    def flush(last=False):
        for batch in ([started[0]] if not last else started):
            for pool in (ID.common, 0, 1, 2, 3):
                mine = [e for e in batch if e[0] == pool]
                if pool == ID.common:
                    for _, _, done in mine:
                        done()
                elif mine:
                    @pl.when(z == pool)
                    def _(mine=mine):
                        for _, _, done in mine:
                            done()
                spare[pool].extend(e[1] for e in mine)
        started[0] = started[1]
        started[1] = []

    def new(count=1):
        first = ids[0]
        ids[0] += count
        return first

    def remote(src, dst, mine, slot, dev):
        src = src() if callable(src) else src
        dst = dst() if callable(dst) else dst
        return pltpu.make_async_remote_copy(
            src_ref=src, dst_ref=dst, send_sem=s.ss.at[mine], recv_sem=s.rs.at[slot],
            device_id=dev, device_id_type=MESH)

    def send(src, dst, slot, dev, cond=None, at=None):
        pool = ID.common if at is None else at
        mine = take(pool)

        def go():
            remote(src, dst, mine, slot, dev).start()

        def done():
            remote(src, dst, mine, slot, dev).wait_send()

        if cond is None:
            go()
            started[1].append((pool, mine, done))
        else:
            pl.when(cond)(go)
            started[1].append((pool, mine, lambda: pl.when(cond)(done)))

    def arrived(dst, slot, cond=None):
        def go():
            remote(dst, dst, 0, slot, (r, z)).wait_recv()

        if cond is None:
            go()
        else:
            pl.when(cond)(go)

    loads = {}

    def load(name, src, dst, k):
        loads[name] = pltpu.make_async_copy(src, dst, s.ls.at[k])
        loads[name].start()

    load(ID.tok, tok_hbm, s.tok_raw, 0)
    load(ID.wqt, wqt_hbm, s.wqt.at[pl.ds(0, 3 * nh * HEAD)], 1)
    load(ID.wo, wo_hbm, s.wo.at[z], 3)
    load(ID.cot, cot_hbm, s.cot_raw, 2)
    load(ID.pw, pw_hbm, s.pw, 4)
    load(ID.fc, fc_hbm, s.fc, 5)

    barrier = pltpu.get_barrier_semaphore()
    for t in range(1, R):
        pl.semaphore_signal(barrier, inc=1, device_id=(lax.rem(r + t, R), z), device_id_type=MESH)

    for t in range(1, T):
        pl.semaphore_signal(barrier, inc=1, device_id=(r, lax.rem(z + t, T)), device_id_type=MESH)
    pl.semaphore_wait(barrier, R + T - 2)

    def find(seq):
        low = jnp.int32(0)
        high = jnp.int32(0)
        for b in range(4):
            same = seq_ref[4 * r + b] == seq
            first = pos_ref[4 * r + b] < R
            low = jnp.where(same & first, b, low)
            high = jnp.where(same & jnp.logical_not(first), b, high)
        return low, high

    def low_pos(rank):
        total = jnp.int32(0)
        for b in range(4):
            here = (seq_ref[4 * rank + b] == c) & (pos_ref[4 * rank + b] < R)
            total = total + jnp.where(here, pos_ref[4 * rank + b], 0)
        return total

    other = find(o)
    own = find(c)
    q_low = (low_pos(2 * g), low_pos(2 * g + 1))

    def swap(raw, k_stage, dst, base):
        for k in range(2):
            s.stage[k_stage, k] = raw[pl.ds(2 * other[k], 2)]
            send(s.stage.at[k_stage, k], dst.at[pl.ds(4 * k + 2 * c, 2)], base + k, (mate, z))
        for k in range(2):
            dst[pl.ds(4 * k + 2 * c, 2)] = raw[pl.ds(2 * own[k], 2)]

    def swapped(dst, base):
        for k in range(2):
            arrived(dst.at[pl.ds(4 * k + 2 * o, 2)], base + k)

    sx = new(4)
    loads[ID.tok].wait()
    swap(s.tok_raw, 0, s.x, sx)

    class Gather:
        def __init__(self, at, pieces, pass_on=None):
            self.at, self.hand = at, pass_on
            self.base = [new(T) for _ in range(pieces)]

        def start(self, u):
            for zz in range(T):
                @pl.when(z == zz)
                def _(zz=zz):
                    a = lambda: self.at(zz, u)
                    if zz < T - 1:
                        send(a, a, self.base[u] + zz, (r, zp), at=zz)
                    if zz > 0:
                        send(a, a, self.base[u] + zz, (r, zm), at=zz)

        def one(self, op, at):
            _, i, u, _ = op
            slot = self.base[u] + i
            a = lambda: self.at(i, u)
            arrived(a, slot)
            if at > i and at < T - 1:
                send(a, a, slot, (r, zp), at=at)
            if at < i and at > 0:
                send(a, a, slot, (r, zm), at=at)
            if self.hand is not None:
                self.hand(i, u, at)

    class Direct:
        def __init__(self, at, pieces):
            self.at = at
            self.base = [new(T) for _ in range(pieces)]

        def start(self, u):
            a = self.at(z, u)
            for t in range(1, T):
                send(a, a, self.base[u] + t, (r, lax.rem(z + t, T)))

        def one(self, op, at):
            _, i, u, _ = op
            arrived(lambda: self.at(i, u), self.base[u] + (at - i) % T)

    def piece(buf, i, u):
        half = 1 if u < SUB else 0
        if SUB == 1:
            return buf.at[4 * half + i]
        return buf.at[4 * half + i, pl.ds(RU * (u % SUB), RU)]

    class Sum:
        def __init__(self, part, from_left, from_right, whole, landing=None):
            self.part, self.fl, self.fr = part, from_left, from_right
            self.whole, self.landing = whole, landing
            self.rl = [new(T + 1) for _ in range(U)]
            self.ag = [new(T) for _ in range(U)]
            self.hand = [new(2) for _ in range(U)] if landing is not None else None

            @pl.when(z == 0)
            def _():
                from_left[0] = jnp.zeros((64, D), BF)
                from_left[4] = jnp.zeros((64, D), BF)

            @pl.when(z == T - 1)
            def _():
                from_right[T - 1] = jnp.zeros((64, D), BF)
                from_right[4 + T - 1] = jnp.zeros((64, D), BF)

        def begin(self, u, ds=(3, 2, 1)):
            @pl.when(z == 0)
            def _():
                for d in ds:
                    send(self.see(self.part, d, u), self.see(self.fl, d, u), self.rl[u] + d, (r, zp), at=0)

            @pl.when(z == T - 1)
            def _():
                for d in ds:
                    e = T - 1 - d
                    send(self.see(self.part, e, u), self.see(self.fr, e, u), self.slot(u, e, T - 2), (r, zm), at=T - 1)

        def slot(self, u, d, to):
            return self.rl[u] + (T if d == to else d)

        def see(self, buf, i, u):
            return lambda: piece(buf, i, u)

        def one(self, op, at):
            kind, i, u, _ = op
            if kind == ID.A:
                slot = self.ag[u] + i
                a = self.see(self.whole, i, u)
                arrived(a, slot)
                if at > i and at < T - 1:
                    send(a, a, slot, (r, zp), at=at)
                if at < i and at > 0:
                    send(a, a, slot, (r, zm), at=at)
                self.pass_on(i, u, at)
                return
            right = kind == ID.R
            buf = self.fl if right else self.fr
            arrived(self.see(buf, i, u), self.rl[u] + i)
            slot = self.rl[u] + i if right else self.slot(u, i, at - 1)
            a = piece(self.part, i, u)
            a[...] = (a[...].astype(F32) + piece(buf, i, u)[...].astype(F32)).astype(BF)
            send(self.see(self.part, i, u), self.see(buf, i, u), slot, (r, zp if right else zm), at=at)

        def spot(self, i, u):
            half = 1 if u < SUB else 0
            if SUB == 1:
                return self.landing.at[half, i % 2]
            return self.landing.at[half, i % 2, pl.ds(RU * (u % SUB), RU)]

        def pass_on(self, i, u, at):
            if self.landing is None:
                return
            send(self.see(self.whole, i, u), lambda: self.spot(i, u), self.hand[u] + i % 2, (mate, z),
                 not_core[i // 2], at=at)

        def last(self, u):
            for at in range(T):
                @pl.when(z == at)
                def _(at=at):
                    if at > 0:
                        arrived(self.see(self.fl, at, u), self.rl[u] + at)
                    if at < T - 1:
                        arrived(self.see(self.fr, at, u), self.rl[u] + T)

        def total(self, index, rows):
            return (self.part[index, rows, :].astype(F32) + self.fl[index, rows, :].astype(F32)
                    + self.fr[index, rows, :].astype(F32))

        def gather(self, u):
            for at in range(T):
                @pl.when(z == at)
                def _(at=at):
                    a = self.see(self.whole, at, u)
                    if at < T - 1:
                        send(a, a, self.ag[u] + at, (r, zp), at=at)
                    if at > 0:
                        send(a, a, self.ag[u] + at, (r, zm), at=at)
                    self.pass_on(at, u, at)

        def handed(self, pieces):
            for u in pieces:
                for k in range(2):
                    arrived(self.spot(k, u), self.hand[u] + k)

    class PlaneSum:
        def __init__(self, part, cut, far, near):
            self.part, self.cut, self.fl, self.near_buf = part, cut, far, near
            self.base = new(max(4, NG))

        def far(self):
            if NG == 4:
                for k in range(2):
                    send(self.part(peers[3], k), self.fl(k), self.base + k, (2 * peers[1 + k] + c, z))

        def near(self, ks=(0, 1)):
            if NG == 4:
                for k in ks:
                    to = peers[2 - k]
                    arrived(self.fl(k), self.base + k)
                    self.cut(to, k)
                    send(self.part(to, None), self.near_buf(2 - k), self.base + 2 + k, (2 * to + c, z))
            else:
                for t in range(1, NG):
                    send(self.part(peers[t], None), self.near_buf(t), self.base + t, (2 * peers[t] + c, z))

        def arrived(self):
            if NG == 4:
                for k in range(2):
                    arrived(self.near_buf(2 - k), self.base + 2 + k)
            else:
                for t in range(1, NG):
                    arrived(self.near_buf(t), self.base + t)

    class PlaneGather:
        def __init__(self, at):
            self.at = at
            self.base = new(max(6, NG))

        def start(self):
            if NG == 4:
                for t, first in ((1, 0), (2, 1)):
                    for leg, half in ((0, first), (1, 1 - first)):
                        a = self.at(g, half)
                        send(a, a, self.base + 2 * (t - 1) + leg, (2 * peers[t] + c, z))
            else:
                for t in range(1, NG):
                    send(self.at(g, None), self.at(g, None), self.base + t, (2 * peers[t] + c, z))

        def relay(self):
            if NG == 4:
                for t, half in ((1, 0), (2, 1)):
                    a = self.at(peers[t], half)
                    arrived(a, self.base + 2 * (t - 1))
                    send(a, a, self.base + 3 + t, (2 * peers[3 - t] + c, z))

        def arrived(self):
            if NG == 4:
                for t, half in ((1, 1), (2, 0)):
                    arrived(self.at(peers[t], half), self.base + 2 * (t - 1) + 1)
                for t, half in ((1, 0), (2, 1)):
                    arrived(self.at(peers[3], half), self.base + 3 + t)
            else:
                for t in range(1, NG):
                    arrived(self.at(sources[t], None), self.base + t)

    WP = nh * HEAD // 4
    swo = new(2 * T)

    def wo_at(i, u, core=None):
        return s.wo.at[i, c if core is None else core, pl.ds(WP * u, WP)]

    def hand_wo(i, u, at):
        send(lambda: wo_at(i, u), lambda: wo_at(i, u), swo + T * u + i, (mate, z), at=at)

    wo_line = Gather(wo_at, 2, hand_wo)
    loads[ID.wo].wait()
    wo_line.start(0)
    wo_line.start(1)
    s.wqt[pl.ds(3 * nh * HEAD, 640 - 3 * nh * HEAD), :] = jnp.zeros((640 - 3 * nh * HEAD, D), BF)
    s.brow[...] = jnp.zeros((1, 640), F32)
    s.brow[:, 0:192] = qvb_ref[0:1, :]
    s.brow[:, 384:576] = qvb_ref[1:2, :]
    g1 = g1_ref[...].reshape(1, -1)
    b1 = b1_ref[...].reshape(1, -1)
    lo_a, hi_a = pl.ds(0, 256), pl.ds(256, 256)

    def project(first):
        for k in range(2):
            for i in range(2):
                j = 4 * k + 2 * first + i
                n, _inv = normed(s.x[j].astype(F32))
                s.act1[j] = (n * g1 + b1).astype(BF)
        a = jnp.concatenate([s.act1[pl.ds(4 * k + 2 * first, 2)].reshape(BLK, D) for k in range(2)], axis=0)
        s.pre[0:256, 0:640] = dg(a, s.wqt[...], 1, 1)
        low = lax.broadcasted_iota(jnp.int32, (BLK, 128), 1) < HEAD
        zero = jnp.zeros((BLK, 128), F32)
        for k in range(2):
            t = [s.pre[BLK * k:BLK * k + BLK, 128 * i:128 * i + 128] + s.brow[:, 128 * i:128 * i + 128]
                 for i in range(5)]
            rows = pl.ds(pl.multiple_of((2 * k + first) * BLK, BLK), BLK)
            s.kv[g, 0, rows, :] = jnp.where(low, roll64(t[1]), roll64(t[3])).astype(BF)
            s.kv[g, 1, rows, :] = jnp.where(low, t[2], t[3]).astype(BF)
            s.kv[g, 2, rows, :] = jnp.where(low, roll64(t[2]), roll64(t[4])).astype(BF)
            s.q[0, rows, :] = (jnp.where(low, t[0], zero) * 0.125).astype(BF)
            s.q[1, rows, :] = (jnp.where(low, roll64(t[0]), zero) * 0.125).astype(BF)
            s.q[2, rows, :] = (jnp.where(low, t[1], zero) * 0.125).astype(BF)

    loads[ID.wqt].wait()
    project(c)
    swapped(s.x, sx)
    project(o)

    skv = new(max(6 * nh, NG))

    def kv_go(h, leg):
        for t, halves in ((1, (lo_a, hi_a)), (2, (hi_a, lo_a))):
            a = s.kv.at[g, h, halves[leg]]
            send(a, a, skv + 6 * h + 2 * (t - 1) + leg, (2 * peers[t] + c, z))

    def kv_relay(h):
        for t, to, half in ((1, 2, lo_a), (2, 1, hi_a)):
            a = s.kv.at[peers[t], h, half]
            arrived(a, skv + 6 * h + 2 * (t - 1))
            send(a, a, skv + 6 * h + 3 + t, (2 * peers[to] + c, z))

    def kv_rest(h):
        for t, half in ((1, hi_a), (2, lo_a)):
            arrived(s.kv.at[peers[t], h, half], skv + 6 * h + 2 * (t - 1) + 1)

    def kv_far(h):
        for t, half in ((1, lo_a), (2, hi_a)):
            arrived(s.kv.at[peers[3], h, half], skv + 6 * h + 3 + t)

    def masks(src):
        k_low = (low_pos(2 * src), low_pos(2 * src + 1))
        i0 = lax.broadcasted_iota(jnp.int32, (256, 256), 0)
        i1 = lax.broadcasted_iota(jnp.int32, (256, 256), 1)

        def token(i, a, b):
            return i + jnp.where(i < BLK, a * BLK, b * BLK - BLK)

        last = 2 * R - 1
        low_mask = jnp.where(token(i0, *k_low) <= token(i1, *q_low), 0.0, NEG)
        high_mask = jnp.where(
            token(i0, last - k_low[0], last - k_low[1])
            <= token(i1, last - q_low[0], last - q_low[1]), 0.0, NEG)
        return low_mask, high_mask

    def all_masks():
        for t in range(4):
            s.mlo[t], s.mhi[t] = masks(peers[t])

    def keys_of(src, h):
        return s.kv[src, h, 0:256, :], s.kv[src, h, 256:512, :]

    def attend(groups, h, fresh=False):
        for half in range(2):
            at = 2 * h + half
            qs = s.q[h, 256 * half:256 * half + 256, :]
            tiles = []
            for src, mlo, mhi in groups:
                klo, khi = keys_of(src, h)
                if half == 0:
                    tiles.append((klo, dg(klo, qs, 1, 1) + mlo[...]))
                else:
                    tiles.append((klo, dg(klo, qs, 1, 1)))
                    tiles.append((khi, dg(khi, qs, 1, 1) + mhi[...]))
            now = None if fresh else s.m[at]
            old = now
            for _, sc in tiles:
                top = jnp.max(sc, axis=0, keepdims=True)
                now = top if now is None else jnp.maximum(now, top)
            total = value = None
            for k, sc in tiles:
                e = jnp.exp(sc - now)
                part = jnp.sum(e, axis=0, keepdims=True)
                total = part if total is None else total + part
                part = dg(k, e.astype(BF), 0, 0)
                value = part if value is None else value + part
            if fresh:
                s.l[at] = total
                s.acc[at] = value
            else:
                f = jnp.exp(old - now)
                s.l[at] = s.l[at] * f + total
                s.acc[at] = s.acc[at] * f + value
            s.m[at] = now

    low = lax.broadcasted_iota(jnp.int32, (256, 128), 1) < HEAD
    low_s = lax.broadcasted_iota(jnp.int32, (BLK, 128), 1) < HEAD

    def settle(h):
        outs = []
        for half in range(2):
            rows = pl.ds(256 * half, 256)
            outs.append(jnp.transpose(s.acc[2 * h + half] / s.l[2 * h + half]))
            s.attp[h, rows, :] = outs[half].astype(BF)
            s.m[2 * h + half] = s.m[2 * h + half] + jnp.log(s.l[2 * h + half])
        if h < nh - 1:
            s.ab[z, h] = jnp.where(low, roll64(outs[0]), outs[1]).astype(BF)
        else:
            for place, half in ((0, 1), (1, 0)):
                v = outs[half]
                s.ab[z, h, BLK * place:BLK * place + BLK, :] = jnp.where(
                    low_s, roll64(v[0:BLK]), v[BLK:256]).astype(BF)

    ab_line = Gather(lambda i, u: s.ab.at[i, u], nh - 1)
    ac_line = Gather(lambda i, u: s.ab.at[i, nh - 1, pl.ds(BLK * u, BLK)], 2)

    sum1 = Sum(s.p1, s.r1, s.l1, s.h)
    sum2 = Sum(s.p2, s.r2, s.l2, s.yo, s.mo)
    sum3 = Sum(s.p3, s.r3, s.l3, s.yg, s.mg)
    s.vsum[...] = jnp.zeros((16, D), F32)

    def upstream():
        swapped(s.cot, sx + 2)
        loads[ID.pw].wait()
        for half in range(2):
            s.ga[256 * half:256 * half + 256, :] = dg(
                s.cot[4 * half:4 * half + 4].reshape(256, D), s.pw[...], 1, 1)

    zeros = jnp.zeros((HEAD, D), BF)

    def pad_own():
        mine = s.wo[z].reshape(nh * HEAD, D)
        for h in range(nh):
            s.wopad[BLK * h:BLK * h + HEAD, :] = zeros
            s.wopad[BLK * h + HEAD:BLK * h + BLK, :] = mine[HEAD * h:HEAD * h + HEAD]

    def pad_all():
        for t in range(1, T):
            for u in range(2):
                arrived(wo_at(lax.rem(z + t, T), u, o), swo + T * u + lax.rem(z + t, T))
        for t in range(T):
            w = s.wo[t].reshape(nh * HEAD, D)
            for h in range(nh):
                part = w[HEAD * h:HEAD * h + HEAD]
                s.wolo[h, t, 0:HEAD, :] = part
                s.wolo[h, t, HEAD:BLK, :] = zeros
                s.wohi[h, t, 0:HEAD, :] = zeros
                s.wohi[h, t, HEAD:BLK, :] = part

    def early_mix():
        for half, w in ((1, s.wohi), (0, s.wolo)):
            total = None
            for h in range(nh - 1):
                a = jnp.concatenate([s.ab[t, h] for t in range(T)], axis=1)
                part = dg(a, w[h].reshape(T * BLK, D), 1, 0)
                total = part if total is None else total + part
            s.pre[256 * half:256 * half + 256, :] = total

    def group(t):
        return peers[t], s.mlo.at[t], s.mhi.at[t]

    def own_keys():
        all_masks()
        for h in range(nh):
            attend([group(0)], h, True)

    def near_keys(h):
        attend([group(1), group(2)], h)

    def far_keys(h):
        kv_far(h)
        attend([group(3)], h)
        settle(h)
        if h < nh - 1:
            ab_line.start(h)
        else:
            ac_line.start(0)
            ac_line.start(1)

    def step_a():
        kv_relay(0)
        kv_go(1, 1)

    def step_b():
        kv_rest(0)
        near_keys(0)

    def step_c():
        kv_relay(1)
        kv_go(2, 0)
        kv_go(2, 1)

    def step_d():
        kv_rest(1)
        near_keys(1)

    def step_e():
        kv_rest(2)
        near_keys(2)

    def whole():
        def one_group(src, fresh):
            s.mlo[0], s.mhi[0] = masks(src)
            for h in range(nh):
                attend([(src, s.mlo.at[0], s.mhi.at[0])], h, fresh)

        one_group(g, True)
        for t in range(1, NG):
            arrived(s.kv.at[sources[t]], skv + t)

        def rest(t, _):
            one_group(lax.rem(g + t, NG), False)
            return 0

        lax.fori_loop(1, NG, rest, 0)
        for h in range(nh):
            settle(h)

    def pads():
        pad_own()
        pad_all()

    g2 = g2_ref[...].reshape(1, -1)
    b2 = b2_ref[...].reshape(1, -1)
    ob = ob_ref[...].reshape(1, -1)
    fcb = fcb_ref[...].reshape(1, -1)
    pb = pb_ref[...].reshape(1, -1)

    def feed(half, total):
        place = 1 - half
        a = jnp.concatenate([s.ab[t, nh - 1, BLK * place:BLK * place + BLK, :] for t in range(T)], axis=1)
        base = 256 * half
        for k, w in ((0, s.wolo), (1, s.wohi)):
            s.pre[base + BLK * k:base + BLK * k + BLK, :] += dg(a, w[nh - 1].reshape(T * BLK, D), 1, 0)

        def norm2(i, _):
            j = 4 * half + i
            rows = pl.ds(pl.multiple_of(base + i * 64, 64), 64)
            x = s.x[j].astype(F32) + s.pre[rows, :] + ob
            s.hid[j] = x
            n, _inv = normed(x)
            s.act2[rows, :] = (n * g2 + b2).astype(BF)
            return 0

        lax.fori_loop(0, 4, norm2, 0)
        part = pl.ds(base, 256)
        s.pre[part, :] = dg(s.act2[part, :], s.fc[...], 1, 0)

        def gelu(i, total):
            rows = pl.ds(pl.multiple_of(base + i * 32, 32), 32)
            v = s.pre[rows, :] + fcb
            square = v * v
            th = jnp.tanh(C0 * (v + C1 * square * v))
            one = 1.0 + th
            s.actd[rows, :] = (0.5 * v * one).astype(BF)
            slope = 0.5 * one + (0.5 * v) * (1.0 - th * th) * (C0 * (1.0 + 3.0 * C1 * square))
            grad = slope * s.ga[rows, :]
            s.gpre[rows, :] = grad.astype(BF)
            return total + fold8(grad)

        total = lax.fori_loop(0, 8, gelu, total)
        s.p1[4 * half:4 * half + 4] = dg(s.gpre[part, :], s.fc[...], 1, 1).astype(BF).reshape(4, 64, D)
        return total

    bias = []

    def feed1():
        loads[ID.fc].wait()
        bias.append(feed(1, jnp.zeros((8, F), F32)))
        for u in range(SUB):
            sum1.begin(u)

    def feed0():
        s.vsum[8:9, :] = jnp.sum(feed(0, bias[0]), axis=0, keepdims=True)
        for u in range(SUB, U):
            sum1.begin(u)

    sw1 = new(2)

    def weight(dst, index, lhs, rhs):
        for i in range(3):
            part = dg(lhs[:, 256 * i:256 * i + 256], rhs, 0, 0).astype(BF)
            lo, hi = 256 * i, 256 * i + 256
            for qd in range(NG):
                a, b = max(lo, qd * Q1), min(hi, qd * Q1 + Q1)
                if a < b:
                    dst[index, qd, a - qd * Q1:b - qd * Q1, :] = part[a - lo:b - lo]

    def add_into(buf, index, extra):
        def body(i, _):
            buf[index, i] = (buf[index, i].astype(F32) + extra[i].astype(F32)).astype(BF)
            return 0

        lax.fori_loop(0, NG, body, 0)

    def weights_a():
        weight(s.w1, 0, s.actd, s.cot[...].reshape(N, D))

    def weights_a2():
        weight(s.w1, 1, s.act2, s.gpre[...])
        send(s.w1.at[o], s.w1r, sw1, (mate, z))

    def plane(part, land, near, whole, size):
        half = size // 2

        def of(buf):
            return lambda i, k: buf.at[c, i] if k is None else buf.at[c, i, pl.ds(half * k, half)]

        def cut(to, k):
            rows = pl.ds(half * k, half)
            part[c, to, rows, :] = (part[c, to, rows, :].astype(F32) + land[k].astype(F32)).astype(BF)

        total = PlaneSum(of(part), cut, lambda k: land.at[k], lambda t: near.at[t])
        share = PlaneGather(of(whole))

        def finish():
            total.arrived()
            step = size // 3

            def body(i, _):
                rows = pl.ds(pl.multiple_of(i * step, step), step)
                v = part[c, g, rows, :].astype(F32)
                for t in got:
                    v = v + near[t, rows, :].astype(F32)
                whole[c, g, rows, :] = v.astype(BF)
                return 0

            lax.fori_loop(0, 3, body, 0)
            share.start()

        return total, share, finish

    got = [1, 2] if NG == 4 else list(range(1, NG))
    total1, share1, finish1 = plane(s.w1, s.w1a, s.w1s, s.w1f, Q1)
    total2, share2, finish2 = plane(s.w2, s.w2a, s.w2s, s.w2f, Q2)

    def weights_b():
        arrived(s.w1r, sw1)
        add_into(s.w1, c, s.w1r)
        total1.far()

    def out_partial():
        for half in range(2):
            base = 256 * half
            s.p2[4 * half:4 * half + 4] = dg(
                s.actd[base:base + 256, :], s.pw[...], 1, 0).astype(BF).reshape(4, 64, D)

    def spans(u):
        half = 1 if u < SUB else 0
        step = min(RU, 32)
        return half, 4 * half + z, [pl.ds(RU * (u % SUB) + step * i, step) for i in range(RU // step)]

    def back2(u):
        sum1.last(u)
        half, index, parts = spans(u)
        sums = [jnp.zeros((8, D), F32)] * 4
        for rows in parts:
            n, inv = normed(s.hid[index, rows, :])
            grad = sum1.total(index, rows)
            up = s.cot[index, rows, :].astype(F32)
            qg = grad * g2
            gh = up + inv * (qg - jnp.mean(qg, axis=-1, keepdims=True)
                             - n * jnp.mean(qg * n, axis=-1, keepdims=True))
            s.gh[half, rows, :] = gh
            s.h[index, rows, :] = gh.astype(BF)
            for k, part in enumerate((grad * n, grad, gh, up)):
                sums[k] = sums[k] + fold8(part)
        sum1.gather(u)
        for k in range(4):
            s.vsum[2 + k:3 + k, :] += jnp.sum(sums[k], axis=0, keepdims=True)

    def slopes(half):
        rows = pl.ds(256 * half, 256)
        grads = dg(s.h[4 * half:4 * half + 4].reshape(256, D), s.wopad[...], 1, 1)
        for h in range(nh):
            d = grads[:, 128 * h:128 * h + 128].astype(BF)
            s.do[h, rows, :] = d
            both = d.astype(F32) * s.attp[h, rows, :].astype(F32)
            s.delta[2 * h + half] = jnp.sum(jnp.transpose(both), axis=0, keepdims=True)

    def tile(k, h, half, mask):
        qs = s.q[h, 256 * half:256 * half + 256, :]
        ds_ = s.do[h, 256 * half:256 * half + 256, :]
        sc = dg(k, qs, 1, 1)
        if mask is not None:
            sc = sc + mask[...]
        p = jnp.exp(sc - s.m[2 * h + half])
        d = p * (dg(k, ds_, 1, 1) - s.delta[2 * h + half])
        p = p.astype(BF)
        d = d.astype(BF)
        return d, dg(d, qs, 1, 0) + dg(p, ds_, 1, 0)

    def back_high(src, mhi, fresh):
        for h in range(nh):
            _, khi = keys_of(src, h)
            d3, k3 = tile(khi, h, 1, mhi)
            s.dk[src, h, 256:512, :] = k3.astype(BF)
            if fresh:
                s.acc[2 * h + 1] = dg(khi, d3, 0, 0)
            else:
                s.acc[2 * h + 1] += dg(khi, d3, 0, 0)

    def back_mid(src, t):
        for h in range(nh):
            klo, _ = keys_of(src, h)
            d2, k2 = tile(klo, h, 1, None)
            s.dkf[t, h] = k2
            s.acc[2 * h + 1] += dg(klo, d2, 0, 0)

    def back_low(src, t, mlo, fresh):
        for h in range(nh):
            klo, _ = keys_of(src, h)
            d1, k1 = tile(klo, h, 0, mlo)
            s.dk[src, h, 0:256, :] = (s.dkf[t, h] + k1).astype(BF)
            if fresh:
                s.acc[2 * h] = dg(klo, d1, 0, 0)
            else:
                s.acc[2 * h] += dg(klo, d1, 0, 0)

    def key_sum(half):
        rows = pl.ds(256 * half, 256)

        def part(i, k):
            return s.dk.at[i, :, rows if k is None else pl.ds(256 * half + BLK * k, BLK)]

        def cut(to, k):
            some = pl.ds(256 * half + BLK * k, BLK)
            for h in range(nh):
                s.dk[to, h, some, :] = (s.dk[to, h, some, :].astype(F32) + s.dka[half, k, h].astype(F32)).astype(BF)

        return PlaneSum(part, cut, lambda k: s.dka.at[half, k], lambda t: s.dkr.at[t, :, rows])

    keys = [key_sum(0), key_sum(1)]

    def finish_output(u):
        sum2.last(u)
        half, index, parts = spans(u)
        for rows in parts:
            s.yo[index, rows, :] = (s.hid[index, rows, :] + sum2.total(index, rows) + pb).astype(BF)
        sum2.gather(u)

    col = [jnp.zeros((1, 128), F32) for _ in range(5)]

    def collect(half):
        keys[half].arrived()
        rows = pl.ds(256 * half, 256)
        dq = [jnp.transpose(s.acc[2 * h + half]) * 0.125 for h in range(nh)]
        dkv = []
        for h in range(nh):
            total = s.dk[g, h, rows, :].astype(F32)
            for t in got:
                total = total + s.dkr[t, h, rows, :].astype(F32)
            dkv.append(total)
        tiles = [
            jnp.where(low, dq[0], roll64(dq[1])),
            jnp.where(low, dq[2], roll64(dkv[0])),
            jnp.where(low, dkv[1], roll64(dkv[2])),
            jnp.where(low, roll64(dkv[0]), dkv[1]),
            jnp.where(low, roll64(dkv[2]), 0.0),
        ]
        for j in range(5):
            col[j] = col[j] + jnp.sum(tiles[j], axis=0, keepdims=True)
            s.gn[rows, 128 * j:128 * j + 128] = tiles[j].astype(BF)
        s.p3[4 * half:4 * half + 4] = dg(s.gn[rows, :], s.wqt[...], 1, 0).astype(BF).reshape(4, 64, D)
        for u in range(SUB) if half == 1 else range(SUB, U):
            sum3.begin(u)

    def put2(first, value, rows):
        done = 0
        while done < rows:
            at, off = divmod(first + done, Q2)
            n = min(Q2 - off, rows - done)
            s.w2[at // NG, at % NG, off:off + n, :] = value[done:done + n].astype(BF)
            done += n

    sw2 = new(2)

    def attention_weight():
        for half in range(2):
            rows = pl.ds(256 * half, 256)
            a = [s.attp[h, rows, :].astype(F32) for h in range(nh)]
            s.attn[rows, 0:128] = jnp.where(low, roll64(a[0]), a[1]).astype(BF)
            s.attn[rows, 128:256] = jnp.where(low, roll64(a[2]), 0.0).astype(BF)
        gout = dg(s.attn[...], s.h[...].reshape(N, D), 0, 0)
        put2(3 * nh * HEAD, gout, nh * HEAD)

    def do_high():
        slopes(1)
        back_high(peers[3], s.mhi.at[3], True)
        keys[1].far()

    def do_low():
        slopes(0)
        back_low(peers[3], 3, s.mlo.at[3], True)
        keys[0].far()

    def mid_low(t):
        back_mid(peers[t], t)
        back_low(peers[t], t, s.mlo.at[t], False)

    def own_hi():
        back_high(g, s.mhi.at[0], False)
        back_mid(g, 0)

    def whole_part():
        slopes(0)
        slopes(1)
        for i in range(2 * nh):
            s.acc[i] = jnp.zeros((128, 256), F32)

        def rest_back(t, _):
            src = lax.rem(g + t, NG)
            s.mlo[0], s.mhi[0] = masks(src)
            back_high(src, s.mhi.at[0], False)
            back_mid(src, 0)
            back_low(src, 0, s.mlo.at[0], False)
            return 0

        lax.fori_loop(0, NG, rest_back, 0)
        for half in (1, 0):
            keys[half].near()

    def weights_c():
        for j in range(5):
            s.vsum[9:10, 128 * j:128 * j + 128] = col[j]
        act1 = s.act1[...].reshape(N, D)
        for j in range(5):
            n = min(128, 3 * nh * HEAD - 128 * j)
            put2(128 * j, dg(s.gn[:, 128 * j:128 * j + 128], act1, 0, 0), n)
        send(s.w2.at[o], s.w2r, sw2, (mate, z))

    def weights_d():
        arrived(s.w2r, sw2)
        add_into(s.w2, c, s.w2r)
        total2.far()

    def back1(u):
        sum3.last(u)
        half, index, parts = spans(u)
        sums = [jnp.zeros((8, D), F32)] * 2
        for rows in parts:
            n, inv = normed(s.x[index, rows, :].astype(F32))
            grad = sum3.total(index, rows)
            qg = grad * g1
            gx = s.gh[half, rows, :] + inv * (qg - jnp.mean(qg, axis=-1, keepdims=True)
                                              - n * jnp.mean(qg * n, axis=-1, keepdims=True))
            s.yg[index, rows, :] = gx.astype(BF)
            for k, part in enumerate((grad * n, grad)):
                sums[k] = sums[k] + fold8(part)
        if u < U - 1:
            sum3.gather(u)
        for k in range(2):
            s.vsum[k:k + 1, :] += jnp.sum(sums[k], axis=0, keepdims=True)
        if u == U - 1:
            s.vz[z] = s.vsum[...].astype(BF)
            v_line.start(0)
            sum3.gather(u)

    v_line = Direct(lambda i, u: s.vz.at[i], 1)
    svc = new(R)
    copies = []

    def give(src, dst):
        copy = pltpu.make_async_copy(src, dst, s.ls.at[6 + len(copies)])
        copy.start()
        copies.append(copy)

    def give_rows(whole, landing, out, halves=(0, 1)):
        for k in halves:
            give(whole.at[pl.ds(4 * k + 2 * c, 2)], out.at[k, c])
            give(landing.at[k], out.at[k, o])

    def outputs_a():
        share1.arrived()
        send(s.w1f.at[c], s.w1f.at[c], sw1 + 1, (mate, z))

    def outputs_b():
        arrived(s.w1f.at[o], sw1 + 1)
        give(s.w1f, w1_out)

    def outputs_o():
        sum2.handed(range(U))
        give_rows(s.yo, s.mo, fo_out)

    def outputs_c():
        share2.arrived()
        send(s.w2f.at[c], s.w2f.at[c], sw2 + 1, (mate, z))

    def give_v():
        for t in range(1, R):
            arrived(s.vc.at[lax.rem(r + R - t, R)], svc + t)
        total = s.vc[0].astype(F32)
        for t in range(1, R):
            total = total + s.vc[t].astype(F32)
        s.vsum[...] = total
        give(s.vsum, v_out)

    def give_w2():
        arrived(s.w2f.at[o], sw2 + 1)
        give(s.w2f, w2_out)

    def give_hi():
        sum3.handed(range(SUB))
        give_rows(s.yg, s.mg, fg_out, (1,))

    def small_sums():
        upper = s.vz[0, 0:8, :].astype(F32)
        for t in range(1, T):
            upper = upper + s.vz[t, 0:8, :].astype(F32)
        s.vc[r] = jnp.concatenate([upper, s.vsum[8:16, :]], axis=0).astype(BF)
        for t in range(1, R):
            send(s.vc.at[r], s.vc.at[r], svc + t, (lax.rem(r + t, R), z))

    def go():
        if NG == 4:
            kv_go(0, 0)
            kv_go(0, 1)
            kv_go(1, 0)
        else:
            for t in range(1, NG):
                send(s.kv.at[g], s.kv.at[g], skv + t, (2 * peers[t] + c, z))
        loads[ID.cot].wait()
        swap(s.cot_raw, 1, s.cot, sx + 2)

    steps = {
        ID.go: go, ID.pads: pads, ID.mix: early_mix, ID.feed1: feed1, ID.feed0: feed0, ID.weights_a: weights_a,
        ID.weights_a2: weights_a2, ID.out_partial: out_partial, ID.weights_b: weights_b, ID.near_w1: total1.near,
        ID.collect1: functools.partial(collect, 1), ID.collect0: functools.partial(collect, 0), ID.finish_w1: finish1,
        ID.aw: attention_weight, ID.weights_c: weights_c, ID.weights_d: weights_d, ID.near_w2: total2.near,
        ID.relay_w1: share1.relay, ID.finish_w2: finish2, ID.relay_w2: share2.relay, ID.pair_w1: outputs_a,
        ID.give_w1: outputs_b, ID.give_o: outputs_o, ID.sums: small_sums, ID.pair_w2: outputs_c, ID.give_v: give_v, ID.give_w2: give_w2, ID.give_hi: give_hi,
        ID.upstream: upstream,
    }
    for u in range(U):
        steps[ID.n2_, u] = functools.partial(back2, u)
        for d in DS:
            steps[ID.begin_out, u, d] = functools.partial(sum2.begin, u, (d,))
        steps[ID.out_, u] = functools.partial(finish_output, u)
        steps[ID.n1_, u] = functools.partial(back1, u)
    if NG == 4:
        steps.update({
            ID.own: own_keys, ID.relay0: step_a, ID.near0: step_b, ID.relay1: step_c,
            ID.far0: functools.partial(far_keys, 0), ID.near1: step_d, ID.relay2: functools.partial(kv_relay, 2),
            ID.far1: functools.partial(far_keys, 1), ID.near2: step_e, ID.far2: functools.partial(far_keys, 2),
            ID.high: do_high, ID.high2: functools.partial(back_high, peers[2], s.mhi.at[2], False),
            ID.high3: functools.partial(back_high, peers[1], s.mhi.at[1], False),
            ID.near_k1a: functools.partial(keys[1].near, (0,)), ID.near_k1b: functools.partial(keys[1].near, (1,)),
            ID.mid3: functools.partial(back_mid, peers[3], 3), ID.low: do_low,
            ID.low2: functools.partial(mid_low, 2), ID.low3: functools.partial(mid_low, 1),
            ID.near_k0a: functools.partial(keys[0].near, (0,)), ID.near_k0b: functools.partial(keys[0].near, (1,)),
            ID.own_hi: own_hi, ID.own_lo: functools.partial(back_low, g, 0, s.mlo.at[0], False),
        })
    else:
        steps.update({
            ID.own: whole, ID.far0: lambda: ab_line.start(0), ID.far1: lambda: ab_line.start(1),
            ID.far2: lambda: (ac_line.start(0), ac_line.start(1)), ID.low: whole_part,
        })
    jobs, marks = timetable(U, T)
    timeline, _ = simulate(T, jobs, marks, LAT)
    emit(T, z, timeline, jobs, marks,
         {ID.wo: wo_line, ID.ab: ab_line, ID.ac: ac_line, ID.ga2: sum1, ID.out: sum2, ID.ga1: sum3, ID.small: v_line}, steps, flush)

    sum3.handed(range(SUB, U))
    give_rows(s.yg, s.mg, fg_out, (0,))
    flush(True)
    assert max(v for k, v in most.items() if k != ID.common) + SPLIT <= (SENDS if NG == 4 else 200)
    assert most[ID.common] <= SPLIT and ids[0] <= (ARRIVALS if NG == 4 else 400)
    for copy in copies:
        copy.wait()


def finish_kernel(R, pos_ref, seq_ref, rank_ref, w1_hbm, w2_hbm, fo_hbm, fg_hbm, v_hbm, out_hbm, gt_hbm,
                  ln1g_ref, ln1b_ref, gq_hbm, gqv_ref, go_hbm, ob_ref, ln2g_ref, ln2b_ref, gf_hbm, fb_ref,
                  gp_hbm, pb_ref, w1_in, w2_in, fo_in, fg_in, v_in, w1_wide, w2_wide, sems, back):
    parts = 4
    D = w2_in.shape[0]
    step = D // parts
    reads = []

    def read(src, dst):
        copy = pltpu.make_async_copy(src, dst, sems.at[len(reads)])
        copy.start()
        reads.append(copy)

    for k in range(parts):
        rows = pl.ds(step * k, step)
        for i in range(2):
            read(w1_hbm.at[i, rows], w1_in.at[i, rows])
        read(w2_hbm.at[rows], w2_in.at[rows])
    read(v_hbm, v_in)
    read(fo_hbm, fo_in)
    read(fg_hbm, fg_in)
    writes = []

    def write(src, dst):
        copy = pltpu.make_async_copy(src, dst, back.at[len(writes)])
        copy.start()
        writes.append(copy)

    for k in range(parts):
        rows = pl.ds(step * k, step)
        for i, dst in enumerate((gp_hbm, gf_hbm)):
            reads[3 * k + i].wait()
            w1_wide[i, rows] = w1_in[i, rows].astype(F32)
            write(w1_wide.at[i, rows], dst.at[rows])
        reads[3 * k + 2].wait()
        w2_wide[rows] = w2_in[rows].astype(F32)
        write(w2_wide.at[rows], gq_hbm.at[rows] if k < parts - 1 else go_hbm)
    for copy in reads[3 * parts:]:
        copy.wait()
    for b in range(4):
        at = 4 * rank_ref[0] + b
        high = jnp.where(pos_ref[at] < R, 0, 1)
        write(fo_in.at[high, seq_ref[at]], out_hbm.at[pl.ds(BLK * b, BLK)])
        write(fg_in.at[high, seq_ref[at]], gt_hbm.at[pl.ds(BLK * b, BLK)])
    for ref, k in ((ln1g_ref, 0), (ln1b_ref, 1), (ln2g_ref, 2), (ln2b_ref, 3), (ob_ref, 4), (pb_ref, 5),
                   (fb_ref, 8)):
        ref[...] = v_in[k:k + 1, :].reshape(-1)
    gqv_ref[0:1, :] = v_in[9:10, 0:192]
    gqv_ref[1:2, :] = v_in[9:10, 384:576]
    for copy in writes:
        copy.wait()


def per_device(R, T, tokens, cotangent, block_pos, block_seq, ln1_gain, ln1_bias, qkv_weight, qv_bias,
               out_weight, out_bias, ln2_gain, ln2_bias, fc_weight, fc_bias, proj_weight, proj_bias):
    D = tokens.shape[1]
    F = fc_weight.shape[1]
    local = qkv_weight.shape[2]
    nh = local // HEAD
    NG = R // 2
    sizes = scratch_list(R, T, D, F, nh)
    names = list(sizes)
    row = lambda v: v
    wqt = jnp.transpose(qkv_weight, (1, 2, 0)).reshape(3 * local, D)
    sm = pl.BlockSpec(memory_space=pltpu.SMEM)
    vm = pl.BlockSpec(memory_space=pltpu.VMEM)
    hb = pl.BlockSpec(memory_space=pl.ANY)
    w1, w2, fo, fg, vs = pl.pallas_call(
        functools.partial(layer_kernel, R, T, D, F, nh, names),
        out_shape=(
            jax.ShapeDtypeStruct((2, NG, D // NG, D), BF),
            jax.ShapeDtypeStruct((2, NG, D // 2 // NG, D), BF),
            jax.ShapeDtypeStruct((2, 2, 2, 64, D), BF),
            jax.ShapeDtypeStruct((2, 2, 2, 64, D), BF),
            jax.ShapeDtypeStruct((16, D), F32),
        ),
        in_specs=[sm, sm, hb, hb, vm, vm, hb, vm, hb, vm, vm, vm, hb, vm, hb, vm],
        out_specs=(hb, hb, hb, hb, hb),
        scratch_shapes=list(sizes.values()),
        compiler_params=pltpu.CompilerParams(
            collective_id=0, has_side_effects=True, vmem_limit_bytes=67043328),
        name="layer",
    )(block_pos, block_seq, tokens.reshape(8, 64, D), cotangent.reshape(8, 64, D), row(ln1_gain),
      row(ln1_bias), wqt, qv_bias, out_weight.reshape(2, local // 2, D), row(out_bias), row(ln2_gain), row(ln2_bias), fc_weight,
      row(fc_bias), proj_weight, row(proj_bias))

    rank = lax.axis_index("ctx").astype(jnp.int32).reshape(1)
    vec = jax.ShapeDtypeStruct((D,), F32)
    outs = pl.pallas_call(
        functools.partial(finish_kernel, R),
        out_shape=(
            jax.ShapeDtypeStruct((4 * BLK, D), BF),
            jax.ShapeDtypeStruct((4 * BLK, D), BF),
            vec, vec,
            jax.ShapeDtypeStruct((3 * local, D), F32),
            jax.ShapeDtypeStruct((2, local), F32),
            jax.ShapeDtypeStruct((local, D), F32),
            vec, vec, vec,
            jax.ShapeDtypeStruct((D, F), F32),
            vec,
            jax.ShapeDtypeStruct((F, D), F32),
            vec,
        ),
        in_specs=[sm, sm, sm, hb, hb, hb, hb, hb],
        out_specs=(hb, hb, vm, vm, hb, vm, hb, vm, vm, vm, hb, vm, hb, vm),
        scratch_shapes=[
            pltpu.VMEM((2, D, D), BF), pltpu.VMEM((D, D), BF), pltpu.VMEM((2, 2, BLK, D), BF),
            pltpu.VMEM((2, 2, BLK, D), BF), pltpu.VMEM((16, D), F32), pltpu.VMEM((2, D, D), F32),
            pltpu.VMEM((D, D), F32), pltpu.SemaphoreType.DMA((16,)), pltpu.SemaphoreType.DMA((20,)),
        ],
        name="finish",
    )(block_pos, block_seq, rank, w1.reshape(2, D, D), w2.reshape(D, D),
      fo.reshape(2, 2, BLK, D), fg.reshape(2, 2, BLK, D), vs)
    (output, grad_tokens, ln1g, ln1b, gq, gqv, go, ob, ln2g, ln2b, gf, fb, gp, pb) = outs
    flat = lambda v: v
    return (output, grad_tokens, flat(ln1g), flat(ln1b),
            jnp.transpose(gq.reshape(3, local, D), (2, 0, 1)), gqv, go, flat(ob), flat(ln2g), flat(ln2b),
            gf, flat(fb), gp, flat(pb))


def solution(mesh):
    R = mesh.shape["ctx"]
    T = mesh.shape["tp"]
    return jax.shard_map(
        functools.partial(per_device, R, T),
        mesh=mesh,
        in_specs=(
            P("ctx", None), P("ctx", None), P(), P(), P(), P(), P(None, None, "tp"), P(None, "tp"),
            P("tp", None), P(), P(), P(), P(None, "tp"), P("tp"), P("tp", None), P(),
        ),
        out_specs=(
            P("ctx", None), P("ctx", None), P(), P(), P(None, None, "tp"), P(None, "tp"), P("tp", None),
            P(), P(), P(), P(None, "tp"), P("tp"), P("tp", None), P(),
        ),
        check_vma=False,
    )
```

profile of v0, /device:TPU:1, one launch (start us, length us, event | category | flops | bytes accessed | tf_op | source)
XLA Modules:
  0.0 124.2 jit_solution(7445646722509539183)
XLA Ops:
  0.7 116.9 %layer.1 = (bf16[2,4,192,768]{3,2,1,0:T(8,128)(2,1)}, bf16[2,4,96,768]{3,2,1,0:T(8,128)(2,1)}, bf16[2,2,2,64,768]{4,3,2,1,0:T(8,128)(2,1)}, bf16[2,2,2,64,768]{4,3,2,1,0:T(8,128)(2,1)}, f32[16,768]{1,0:T(8,128)}) custom-call(s32[32]{0:T(128)} %pos_ref.1, s32[32]{0:T(128)} %seq_ref.1, bf16[8,64,768]{2,1,0:T(8,128)(2,1)} %bitcast.17, ...), custom_call_target="tpu_custom_call" | custom-call | tf_op jit(solution)/shard_map/layer/pallas_call | solution.py:1489
  117.5 6.5 %finish.1 = (bf16[512,768]{1,0:T(8,128)(2,1)}, bf16[512,768]{1,0:T(8,128)(2,1)}, f32[768]{0:T(1024)}, f32[768]{0:T(1024)}, f32[576,768]{1,0:T(8,128)}, /*index=5...) custom-call(s32[32]{0:T(128)} %pos_ref.1, ...), custom_call_target="tpu_custom_call" | custom-call | tf_op jit(solution)/shard_map/finish/pallas_call | solution.py:1510
where the time goes:
time: 124 us
  Pallas kernels  123 us (99%)
    pallas_call x1, Pallas kernels, per_device(): pl.pallas_call(functools.partial(layer_kernel, R, T, D, F, nh, names), ou...  117 us
    pallas_call x1, Pallas kernels, per_device(): pl.pallas_call(functools.partial(finish_kernel, R), out_shape=(jax.ShapeD...  6.5 us

commit v1 on v0

--- a/solution.py
+++ b/solution.py
@@ -24,12 +24,12 @@
 C0 = 0.7978845608028654
 C1 = 0.044715
 U = 4
-SENDS = 90
-SPLIT_AT = 26
-ARRIVALS = 222
-TIDY = (ID.far1, ID.feed1, ID.weights_b, ID.high, ID.low3, ID.collect0, (ID.n1_, 2))
-
-LAT = 1.6
+SENDS = 74
+SPLIT_AT = 22
+ARRIVALS = 174
+TIDY = (ID.far1, ID.feed1, ID.weights_b, (ID.n2_, 2), ID.high, ID.low, ID.low3, ID.collect1, ID.collect0, (ID.n1_, 0), (ID.n1_, 2))
+
+LAT = 2.0
 OUT_FROM = 15.0
 OUT_GAP = 1.0
 DS = (3, 2, 1)
@@ -73,16 +73,22 @@
         free[z, step] = begin + tau
         inbox[z + step].append((begin + tau + lat, op))
 
+    transit = []
+
+    def cross(entry):
+        time, z, to, op = entry
+        step = 1 if to > z else -1
+        tau = jobs[op[3]][0][op[2]]
+        begin = max(time, free.get((z, step), 0.0))
+        free[z, step] = begin + tau
+        if z + step == to:
+            inbox[to].append((begin + tau + lat, op))
+        else:
+            transit.append((begin + 0.7, z + step, to, op))
+
     def spread(time, z, op):
         if jobs[op[3]][4]:
-            for to in range(T):
-                step = 1 if to > z else -1
-                begin = time
-                for k in range(z, to, step):
-                    begin = max(begin + (0.7 if k != z else 0.0), free.get((k, step), 0.0))
-                    free[k, step] = begin + jobs[op[3]][0][op[2]]
-                if to != z:
-                    inbox[to].append((begin + jobs[op[3]][0][op[2]] + lat, op))
+            transit.extend((time, z, to, op) for to in range(T) if to != z)
             return
         if z >= op[1] and z < T - 1:
             post(time, z, 1, op)
@@ -123,6 +129,10 @@
 
     while True:
         best = None
+        for entry in transit:
+            key = (entry[0], -1, entry[1], entry[2])
+            if best is None or key < best[0]:
+                best = (key, entry[1], (ID.cross, entry))
         for z in range(T):
             for entry in list(inbox[z]):
                 if passive(z, entry[1]):
@@ -144,6 +154,10 @@
         if best is None:
             break
         key, z, item = best
+        if item[0] == ID.cross:
+            transit.remove(item[1])
+            cross(item[1])
+            continue
         begin = start_of(z, item)
         if item[0] == ID.op:
             _, op = item[1]
@@ -176,7 +190,7 @@
         spots = {name: sum(t for z in range(T) for t, op in out[z] if op == (ID.M, name)) for name in marks}
         assert all(len(l) == 0 for l in left), left
         return simulate(T, jobs, marks, lat, sorted(marks, key=lambda n: spots[n]))
-    assert all(len(l) == 0 for l in left) and all(len(i) == 0 for i in inbox), (left, inbox)
+    assert all(len(l) == 0 for l in left) and all(len(i) == 0 for i in inbox + [transit]), (left, inbox)
     return out, max(now)
 
 def emit(T, z, timeline, jobs, marks, actors, steps, flush):
@@ -215,7 +229,7 @@
         ID.wo: ([1.65] * 2, False, True, 0, False), ID.ab: ([1.5] * 2, False, True, 0, False),
         ID.ac: ([0.8] * 2, False, True, 0, False), ID.ga2: ([tau] * U, True, True, 0, False),
         ID.out: ([tau] * U, True, False, 1, False), ID.ga1: ([tau] * U, True, False, 0, False),
-        ID.small: ([0.5], False, False, 0, True),
+        ID.small: ([0.5], False, False, 1, True),
     }
     m = {}
 
@@ -255,7 +269,7 @@
                  posts=[(ID.out, u, (d,))], low=1)
         step((ID.out_, u), 0.2, needs=sums(ID.out), posts=[(ID.out, u, ID.gather)], low=1)
         step((ID.n1_, u), norm, needs=sums(ID.ga1), posts=[(ID.ga1, u, ID.gather)])
-    m[(ID.n1_, U - 1)][ID.posts].insert(0, (ID.small, 0, ID.gather))
+    step(ID.norm_sums, 1.8, [(ID.weights_c, 0)], posts=[(ID.small, 0, ID.gather)], low=1)
     step(ID.high, 1.4, needs=every(ID.ga2, hi))
     step(ID.high2, 0.9, [(ID.high, 0)])
     step(ID.near_k1a, 0.15, [(ID.high, 3.4), (ID.high2, 0)])
@@ -567,7 +581,7 @@
             self.part, self.fl, self.fr = part, from_left, from_right
             self.whole, self.landing = whole, landing
             self.rl = [new(T + 1) for _ in range(U)]
-            self.ag = [new(T) for _ in range(U)]
+            self.ag = self.rl
             self.hand = [new(2) for _ in range(U)] if landing is not None else None
 
             @pl.when(z == 0)
@@ -1211,7 +1225,9 @@
         for j in range(5):
             col[j] = col[j] + jnp.sum(tiles[j], axis=0, keepdims=True)
             s.gn[rows, 128 * j:128 * j + 128] = tiles[j].astype(BF)
-        s.p3[4 * half:4 * half + 4] = dg(s.gn[rows, :], s.wqt[...], 1, 0).astype(BF).reshape(4, 64, D)
+        back = dg(s.gn[rows, :], s.wqt[...], 1, 0)
+        s.p3[4 * half:4 * half + 4] = back.astype(BF).reshape(4, 64, D)
+        s.ga[rows, 0:D] = back
         for u in range(SUB) if half == 1 else range(SUB, U):
             sum3.begin(u)
 
@@ -1287,25 +1303,27 @@
     def back1(u):
         sum3.last(u)
         half, index, parts = spans(u)
-        sums = [jnp.zeros((8, D), F32)] * 2
         for rows in parts:
             n, inv = normed(s.x[index, rows, :].astype(F32))
-            grad = sum3.total(index, rows)
-            qg = grad * g1
+            qg = sum3.total(index, rows) * g1
             gx = s.gh[half, rows, :] + inv * (qg - jnp.mean(qg, axis=-1, keepdims=True)
                                               - n * jnp.mean(qg * n, axis=-1, keepdims=True))
             s.yg[index, rows, :] = gx.astype(BF)
-            for k, part in enumerate((grad * n, grad)):
-                sums[k] = sums[k] + fold8(part)
-        if u < U - 1:
-            sum3.gather(u)
+        sum3.gather(u)
+
+    def norm_sums():
+        def body(i, sums):
+            n, _inv = normed(s.x[i].astype(F32))
+            grad = s.ga[pl.ds(pl.multiple_of(i * 64, 64), 64), 0:D]
+            return sums[0] + fold8(grad * n), sums[1] + fold8(grad)
+
+        sums = lax.fori_loop(0, 8, body, (z8, z8))
         for k in range(2):
-            s.vsum[k:k + 1, :] += jnp.sum(sums[k], axis=0, keepdims=True)
-        if u == U - 1:
-            s.vz[z] = s.vsum[...].astype(BF)
-            v_line.start(0)
-            sum3.gather(u)
-
+            s.vsum[k:k + 1, :] = jnp.sum(sums[k], axis=0, keepdims=True)
+        s.vz[z] = s.vsum[...].astype(BF)
+        v_line.start(0)
+
+    z8 = jnp.zeros((8, D), F32)
     v_line = Direct(lambda i, u: s.vz.at[i], 1)
     svc = new(R)
     copies = []
@@ -1378,7 +1396,7 @@
         ID.collect1: functools.partial(collect, 1), ID.collect0: functools.partial(collect, 0), ID.finish_w1: finish1,
         ID.aw: attention_weight, ID.weights_c: weights_c, ID.weights_d: weights_d, ID.near_w2: total2.near,
         ID.relay_w1: share1.relay, ID.finish_w2: finish2, ID.relay_w2: share2.relay, ID.pair_w1: outputs_a,
-        ID.give_w1: outputs_b, ID.give_o: outputs_o, ID.sums: small_sums, ID.pair_w2: outputs_c, ID.give_v: give_v, ID.give_w2: give_w2, ID.give_hi: give_hi,
+        ID.give_w1: outputs_b, ID.give_o: outputs_o, ID.sums: small_sums, ID.norm_sums: norm_sums, ID.pair_w2: outputs_c, ID.give_v: give_v, ID.give_w2: give_w2, ID.give_hi: give_hi,
         ID.upstream: upstream,
     }
     for u in range(U):
@@ -1422,7 +1440,7 @@
 def finish_kernel(R, pos_ref, seq_ref, rank_ref, w1_hbm, w2_hbm, fo_hbm, fg_hbm, v_hbm, out_hbm, gt_hbm,
                   ln1g_ref, ln1b_ref, gq_hbm, gqv_ref, go_hbm, ob_ref, ln2g_ref, ln2b_ref, gf_hbm, fb_ref,
                   gp_hbm, pb_ref, w1_in, w2_in, fo_in, fg_in, v_in, w1_wide, w2_wide, sems, back):
-    parts = 4
+    parts = 2
     D = w2_in.shape[0]
     step = D // parts
     reads = []
@@ -1455,7 +1473,9 @@
             write(w1_wide.at[i, rows], dst.at[rows])
         reads[3 * k + 2].wait()
         w2_wide[rows] = w2_in[rows].astype(F32)
-        write(w2_wide.at[rows], gq_hbm.at[rows] if k < parts - 1 else go_hbm)
+        low, most = step * k, min(step * k + step, gq_hbm.shape[0])
+        write(w2_wide.at[pl.ds(low, most - low)], gq_hbm.at[pl.ds(low, most - low)])
+    write(w2_wide.at[pl.ds(most, D - most)], go_hbm)
     for copy in reads[3 * parts:]:
         copy.wait()
     for b in range(4):
@@ -1527,7 +1547,7 @@
         scratch_shapes=[
             pltpu.VMEM((2, D, D), BF), pltpu.VMEM((D, D), BF), pltpu.VMEM((2, 2, BLK, D), BF),
             pltpu.VMEM((2, 2, BLK, D), BF), pltpu.VMEM((16, D), F32), pltpu.VMEM((2, D, D), F32),
-            pltpu.VMEM((D, D), F32), pltpu.SemaphoreType.DMA((16,)), pltpu.SemaphoreType.DMA((20,)),
+            pltpu.VMEM((D, D), F32), pltpu.SemaphoreType.DMA((9,)), pltpu.SemaphoreType.DMA((15,)),
         ],
         name="finish",
     )(block_pos, block_seq, rank, w1.reshape(2, D, D), w2.reshape(D, D),

time: 124 us -> 122 us (0.984)
  Pallas kernels: 123 us -> 121 us
    pallas_call x1, Pallas kernels: 117 us -> 115 us  [per_device(): pl.pallas_call(functools.partial(layer_kernel, R, T, D, F, nh, names), ou...]
where the time goes in v1:
time: 122 us
  Pallas kernels  121 us (99%)
    pallas_call x1, Pallas kernels, per_device(): pl.pallas_call(functools.partial(layer_kernel, R, T, D, F, nh, names), ou...  115 us
    pallas_call x1, Pallas kernels, per_device(): pl.pallas_call(functools.partial(finish_kernel, R), out_shape=(jax.ShapeD...  6.06 us

profile of v1, /device:TPU:1, one launch (start us, length us, event | category | flops | bytes accessed | tf_op | source)
XLA Modules:
  0.0 122.0 jit_solution(17204265395750605515)
XLA Ops:
  0.7 115.1 %layer.1 = (bf16[2,4,192,768]{3,2,1,0:T(8,128)(2,1)}, bf16[2,4,96,768]{3,2,1,0:T(8,128)(2,1)}, bf16[2,2,2,64,768]{4,3,2,1,0:T(8,128)(2,1)}, bf16[2,2,2,64,768]{4,3,2,1,0:T(8,128)(2,1)}, f32[16,768]{1,0:T(8,128)}) custom-call(s32[32]{0:T(128)} %pos_ref.1, s32[32]{0:T(128)} %seq_ref.1, bf16[8,64,768]{2,1,0:T(8,128)(2,1)} %bitcast.17, ...), custom_call_target="tpu_custom_call" | custom-call | tf_op jit(solution)/shard_map/layer/pallas_call | solution.py:1509
  115.7 6.1 %finish.1 = (bf16[512,768]{1,0:T(8,128)(2,1)}, bf16[512,768]{1,0:T(8,128)(2,1)}, f32[768]{0:T(1024)}, f32[768]{0:T(1024)}, f32[576,768]{1,0:T(8,128)}, /*index=5...) custom-call(s32[32]{0:T(128)} %pos_ref.1, ...), custom_call_target="tpu_custom_call" | custom-call | tf_op jit(solution)/shard_map/finish/pallas_call | solution.py:1530

commit v2 on v1

--- a/solution.py
+++ b/solution.py
@@ -24,13 +24,13 @@
 C0 = 0.7978845608028654
 C1 = 0.044715
 U = 4
-SENDS = 74
+SENDS = 70
 SPLIT_AT = 22
-ARRIVALS = 174
+ARRIVALS = 154
 TIDY = (ID.far1, ID.feed1, ID.weights_b, (ID.n2_, 2), ID.high, ID.low, ID.low3, ID.collect1, ID.collect0, (ID.n1_, 0), (ID.n1_, 2))
 
-LAT = 2.0
-OUT_FROM = 15.0
+LAT = 2.3
+OUT_FROM = 14.0
 OUT_GAP = 1.0
 DS = (3, 2, 1)
 
@@ -276,10 +276,12 @@
     step(ID.high3, 0.9, [(ID.high2, 0)])
     step(ID.near_k1b, 0.15, [(ID.near_k1a, 0), (ID.high3, 0)])
     step(ID.mid3, 0.9, [(ID.high3, 0)])
+    step(ID.mid2, 0.9, [(ID.mid3, 0)])
+    step(ID.mid1, 0.9, [(ID.mid2, 0)])
     step(ID.low, 1.4, [(ID.mid3, 0), (ID.near_k1b, 0)], every(ID.ga2, lo))
-    step(ID.low2, 1.7, [(ID.low, 0)])
+    step(ID.low2, 0.9, [(ID.low, 0), (ID.mid2, 0)])
     step(ID.near_k0a, 0.15, [(ID.low, 3.4), (ID.low2, 0)])
-    step(ID.low3, 1.7, [(ID.low2, 0)])
+    step(ID.low3, 0.9, [(ID.low2, 0), (ID.mid1, 0)])
     step(ID.near_k0b, 0.15, [(ID.near_k0a, 0), (ID.low3, 0)])
     step(ID.own_hi, 1.7, [(ID.low3, 0)])
     step(ID.collect1, 0.9, [(ID.own_hi, 0), (ID.near_k1b, 7.0)], posts=[(ID.ga1, u, DS) for u in hi])
@@ -577,10 +579,10 @@
         return buf.at[4 * half + i, pl.ds(RU * (u % SUB), RU)]
 
     class Sum:
-        def __init__(self, part, from_left, from_right, whole, landing=None):
+        def __init__(self, part, from_left, from_right, whole, landing=None, slots=None):
             self.part, self.fl, self.fr = part, from_left, from_right
             self.whole, self.landing = whole, landing
-            self.rl = [new(T + 1) for _ in range(U)]
+            self.rl = [new(T + 1) for _ in range(U)] if slots is None else slots
             self.ag = self.rl
             self.hand = [new(2) for _ in range(U)] if landing is not None else None
 
@@ -880,7 +882,7 @@
 
     sum1 = Sum(s.p1, s.r1, s.l1, s.h)
     sum2 = Sum(s.p2, s.r2, s.l2, s.yo, s.mo)
-    sum3 = Sum(s.p3, s.r3, s.l3, s.yg, s.mg)
+    sum3 = Sum(s.p3, s.r3, s.l3, s.yg, s.mg, sum1.rl)
     s.vsum[...] = jnp.zeros((16, D), F32)
 
     def upstream():
@@ -1260,10 +1262,6 @@
         back_low(peers[3], 3, s.mlo.at[3], True)
         keys[0].far()
 
-    def mid_low(t):
-        back_mid(peers[t], t)
-        back_low(peers[t], t, s.mlo.at[t], False)
-
     def own_hi():
         back_high(g, s.mhi.at[0], False)
         back_mid(g, 0)
@@ -1414,7 +1412,9 @@
             ID.high3: functools.partial(back_high, peers[1], s.mhi.at[1], False),
             ID.near_k1a: functools.partial(keys[1].near, (0,)), ID.near_k1b: functools.partial(keys[1].near, (1,)),
             ID.mid3: functools.partial(back_mid, peers[3], 3), ID.low: do_low,
-            ID.low2: functools.partial(mid_low, 2), ID.low3: functools.partial(mid_low, 1),
+            ID.mid2: functools.partial(back_mid, peers[2], 2), ID.mid1: functools.partial(back_mid, peers[1], 1),
+            ID.low2: functools.partial(back_low, peers[2], 2, s.mlo.at[2], False),
+            ID.low3: functools.partial(back_low, peers[1], 1, s.mlo.at[1], False),
             ID.near_k0a: functools.partial(keys[0].near, (0,)), ID.near_k0b: functools.partial(keys[0].near, (1,)),
             ID.own_hi: own_hi, ID.own_lo: functools.partial(back_low, g, 0, s.mlo.at[0], False),
         })

time: 122 us -> 121 us (level)
  no operation moved by 1% of the time
where the time goes in v2:
time: 121 us
  Pallas kernels  120 us (99%)
    pallas_call x1, Pallas kernels, per_device(): pl.pallas_call(functools.partial(layer_kernel, R, T, D, F, nh, names), ou...  114 us
    pallas_call x1, Pallas kernels, per_device(): pl.pallas_call(functools.partial(finish_kernel, R), out_shape=(jax.ShapeD...  6.06 us

profile of v2, /device:TPU:1, one launch (start us, length us, event | category | flops | bytes accessed | tf_op | source)
XLA Modules:
  0.0 120.8 jit_solution(14888254329797134379)
XLA Ops:
  0.7 113.9 %layer.1 = (bf16[2,4,192,768]{3,2,1,0:T(8,128)(2,1)}, bf16[2,4,96,768]{3,2,1,0:T(8,128)(2,1)}, bf16[2,2,2,64,768]{4,3,2,1,0:T(8,128)(2,1)}, bf16[2,2,2,64,768]{4,3,2,1,0:T(8,128)(2,1)}, f32[16,768]{1,0:T(8,128)}) custom-call(s32[32]{0:T(128)} %pos_ref.1, s32[32]{0:T(128)} %seq_ref.1, bf16[8,64,768]{2,1,0:T(8,128)(2,1)} %bitcast.17, ...), custom_call_target="tpu_custom_call" | custom-call | tf_op jit(solution)/shard_map/layer/pallas_call | solution.py:1509
  114.6 6.1 %finish.1 = (bf16[512,768]{1,0:T(8,128)(2,1)}, bf16[512,768]{1,0:T(8,128)(2,1)}, f32[768]{0:T(1024)}, f32[768]{0:T(1024)}, f32[576,768]{1,0:T(8,128)}, /*index=5...) custom-call(s32[32]{0:T(128)} %pos_ref.1, ...), custom_call_target="tpu_custom_call" | custom-call | tf_op jit(solution)/shard_map/finish/pallas_call | solution.py:1530
